TPU v7x, 32 devices: a whole 2x2x4 slice. The times are simulated.
32 devices in a mesh: section: 4 (over y, core), row: 8 (over z, x).
Axes of the slice: x: 2, y: 2, z: 4, core: 2. Of those that a mesh axis runs over, the one named last changes fastest.
Arguments:
- diag_blocks: float32 [4, 2, 8, 256, 256], P('section', None, 'row'), may hold values from -9 to 9, as said below
- coupling_blocks: float32 [4, 2, 8, 256, 256], P('section', None, 'row'), as said below
Outputs:
- reduced_diag: float32 [4, 2, 8, 256, 256], P('section', None, 'row')
- reduced_coupling: float32 [4, 2, 8, 256, 256], P('section', None, 'row')
Inputs may be any that keep to these rules, and one draw needn't show every extreme that they name: `diag_blocks`: every block is symmetric. `coupling_blocks`: every block is three times the identity plus a random part whose entries are at most 5 / sqrt(256) in magnitude and whose spectral norm is at most 2.5, so every block is invertible.
All inputs are finite; a program needn't handle non-finite values.
Results may differ from a plain program's by a relative error of at most 0.0003.
Values sent between devices are 32-bit elements; how exact they have to be, the bound alone decides.
A program may use at most 64 MiB of HBM per device.

v0:
```python
import jax
import jax.numpy as jnp
from jax import lax
from jax.sharding import PartitionSpec as P

highest = lax.Precision.HIGHEST


def shifted(block, axis, distance):
    devices = range(lax.axis_size(axis))
    route = [(i - distance, i) for i in devices if i - distance in devices]
    return lax.ppermute(block, axis, route)


def product(left, right):
    return jnp.dot(left, right, precision=highest, preferred_element_type=jnp.float32)


def qfactor(panel_now):
    gram_first = product(panel_now.T, panel_now)
    lower_first = jnp.linalg.cholesky(gram_first)
    first_pass = jax.scipy.linalg.solve_triangular(lower_first, panel_now.T, lower=True).T
    gram_second = product(first_pass.T, first_pass)
    lower_second = jnp.linalg.cholesky(gram_second)
    orthogonal = jax.scipy.linalg.solve_triangular(lower_second, first_pass.T, lower=True).T
    upper_part = product(lower_second.T, lower_first.T)
    return (orthogonal, upper_part)


def segment(panel_now, diagonal):
    orthogonal, upper_part = qfactor(panel_now)
    new_diag = [product(product(orthogonal.T, diagonal[0]), orthogonal)]
    triangles = [upper_part]
    return (jnp.stack(new_diag), jnp.stack(triangles), orthogonal)


def pass_on(outgoing):
    return shifted(outgoing, "row", 1)


def shards(diag_blocks, coupling_blocks):
    diagonal = diag_blocks[0]
    coupling = coupling_blocks[0]
    batch_count = diagonal.shape[0]
    row_count = lax.axis_size("row")
    position = lax.axis_index("row")
    leading = position == 0

    def opening(incoming, own_first):
        made = product(own_first, incoming)
        return jnp.where(leading, own_first, made)

    new_start = jnp.zeros_like(diagonal)
    tri_start = jnp.zeros_like(diagonal)

    def process_one(incoming, new_all, tri_all, clipped):
        diag_now = lax.dynamic_index_in_dim(diagonal, clipped, 0, keepdims=False)
        coupling_now = lax.dynamic_index_in_dim(coupling, clipped, 0, keepdims=False)
        first_panel = opening(incoming, coupling_now[0])
        new_diag, triangles, last_factor = segment(first_panel, diag_now)
        new_all = lax.dynamic_update_index_in_dim(new_all, new_diag, clipped, 0)
        tri_all = lax.dynamic_update_index_in_dim(tri_all, triangles, clipped, 0)
        return (new_all, tri_all, last_factor)

    def round_step(step_number, carried):
        incoming, new_all, tri_all, outgoing = carried
        batch_index = step_number - position
        active = (batch_index >= 0) & (batch_index < batch_count)
        clipped = jnp.clip(batch_index, 0, batch_count - 1)
        new_all, tri_all, outgoing = lax.cond(
            active,
            lambda: process_one(incoming, new_all, tri_all, clipped),
            lambda: (new_all, tri_all, outgoing),
        )
        return (pass_on(outgoing), new_all, tri_all, outgoing)

    message_start = jnp.zeros_like(coupling[0, 0])
    carried = lax.fori_loop(
        0,
        row_count + batch_count - 1,
        round_step,
        (message_start, new_start, tri_start, message_start),
    )
    return (carried[1][None], carried[2][None])


def solution(mesh):
    placed = (P("section", None, "row", None, None), P("section", None, "row", None, None))
    return jax.shard_map(
        shards,
        mesh=mesh,
        in_specs=placed,
        out_specs=(P("section", None, "row", None, None), P("section", None, "row", None, None)),
        check_vma=False,
    )
```

profile of v0, /device:TPU:26, one launch (start us, length us, event | category | flops | bytes accessed | tf_op | source)
XLA Modules:
  0.0 1206.7 jit_solution(1754750417579483523)
XLA Ops:
  0.7 0.8 broadcast.74.clone
  2.1 1203.8 %while.25 = (s32[]{:T(128)}, f32[256,256]{0,1:T(8,128)S(1)}, f32[2,1,256,256]{3,2,1,0:T(8,128)S(1)}, f32[2,1,256,256]{3,2,1,0:T(8,128)}, f32[256,256]{0,1:T(8,12...) while((s32[]{:T(128)}, f32[256,256]{0,1:T(8,128)S(1)}, ...), condition=%wide.region_7.10_spmd, body=%wide.region_0.0_spmd.sunk | while | flops 1612481024 | bytes 19142408 | solution.py:78
  2.1 1.3 collective-permute-start
  3.4 8.6 collective-permute-done
  12.0 1.3 collective-permute-start
  13.3 7.8 collective-permute-done
  21.1 1.3 collective-permute-start
  22.4 7.5 collective-permute-done
  29.9 1.3 collective-permute-start
  31.2 7.6 collective-permute-done
  38.8 1.3 collective-permute-start
  40.1 7.9 collective-permute-done
  48.0 1.3 collective-permute-start
  49.3 7.9 collective-permute-done
  57.1 1.3 collective-permute-start
  58.4 878.7 %collective-permute-done = f32[256,256]{0,1:T(8,128)S(1)} collective-permute-done((f32[256,256]{0,1:T(8,128)S(1)}, f32[256,256]{0,1:T(8,128)S(1)}, u32[]{:S(2)}, u32[]{:S(2)}) %collective-permute-start) | collective-permute-done | bytes 262176 | tf_op jit(solution)/shard_map/while/body/eval_jaxpr/ppermute | solution.py:12
  937.1 125.7 %conditional.2 = ((f32[2,1,256,256]{3,2,1,0:T(8,128)S(1)}, f32[2,1,256,256]{3,2,1,0:T(8,128)}, f32[256,256]{0,1:T(8,128)S(1)})) conditional(s32[]{:T(128)} %convert_element_type.8, (f32[2,1,256,256]{3,2,1,0:T(8,128)S(1)}, f32[2,1,256,256]{3,2,1,0:T(8,128)}, f32[256,256]{0,1:T(8,128)S(1)}) %tuple.76, (pred[]{:T(512)}, s32[]{:T(128)}, ...), branch_computations={%region_1.1_spmd, %region_2.0_spmd} | conditional | flops 1612481024 | bytes 18093556 | solution.py:70
  938.3 11.7 cholesky.130
  950.0 9.8 custom-call.13
  960.4 11.7 cholesky.147
  972.1 0.7 compare_reduce_fusion.2
  974.1 3.8 while.23
  974.7 1.3 bitcast_dynamic-update-slice_fusion.4
  976.0 0.6 fusion.66
  976.6 1.3 bitcast_dynamic-update-slice_fusion.4
  977.9 19.7 %custom-call.14 = f32[2,128,128]{1,2,0:T(8,128)S(1)} custom-call(f32[2,128,128]{2,1,0:T(8,128)S(1)} %get-tuple-element.215), custom_call_target="InvertDiagBlocksLowerTriangular" | custom-call | tf_op jit(solution)/shard_map/while/body/eval_jaxpr/cond/branch_1_fun/jit(_solve_triangular)/triangular_solve | solution.py:22
  999.2 11.7 cholesky.164
  1011.0 9.8 custom-call.15
  1021.3 11.7 cholesky.181
  1033.0 0.6 compare_reduce_fusion
  1033.7 0.6 compare_reduce_fusion.1
  1035.5 3.8 while.24
  1035.6 0.6 fusion.67
  1036.2 1.3 bitcast_dynamic-update-slice_fusion.5
  1038.1 1.3 bitcast_dynamic-update-slice_fusion.5
  1039.3 19.7 %custom-call.16 = f32[2,128,128]{1,2,0:T(8,128)S(1)} custom-call(f32[2,128,128]{2,1,0:T(8,128)S(1)} %get-tuple-element.216), custom_call_target="InvertDiagBlocksLowerTriangular" | custom-call | tf_op jit(solution)/shard_map/while/body/eval_jaxpr/cond/branch_1_fun/jit(_solve_triangular)/triangular_solve | solution.py:25
  1060.0 0.7 copy-done.3
  1061.2 0.8 copy-done.4
  1062.8 1.3 collective-permute-start
  1064.1 7.9 collective-permute-done
  1071.9 125.7 %conditional.2 = ((f32[2,1,256,256]{3,2,1,0:T(8,128)S(1)}, f32[2,1,256,256]{3,2,1,0:T(8,128)}, f32[256,256]{0,1:T(8,128)S(1)})) conditional(s32[]{:T(128)} %convert_element_type.8, (f32[2,1,256,256]{3,2,1,0:T(8,128)S(1)}, f32[2,1,256,256]{3,2,1,0:T(8,128)}, f32[256,256]{0,1:T(8,128)S(1)}) %tuple.76, (pred[]{:T(512)}, s32[]{:T(128)}, ...), branch_computations={%region_1.1_spmd, %region_2.0_spmd} | conditional | flops 1612481024 | bytes 18093556 | solution.py:70
  1073.2 11.7 cholesky.130
  1084.9 9.8 custom-call.13
  1095.2 11.7 cholesky.147
  1107.0 0.7 compare_reduce_fusion.2
  1108.9 3.8 while.23
  1109.0 0.6 fusion.66
  1109.6 1.3 bitcast_dynamic-update-slice_fusion.4
  1111.5 1.3 bitcast_dynamic-update-slice_fusion.4
  1112.7 19.7 %custom-call.14 = f32[2,128,128]{1,2,0:T(8,128)S(1)} custom-call(f32[2,128,128]{2,1,0:T(8,128)S(1)} %get-tuple-element.215), custom_call_target="InvertDiagBlocksLowerTriangular" | custom-call | tf_op jit(solution)/shard_map/while/body/eval_jaxpr/cond/branch_1_fun/jit(_solve_triangular)/triangular_solve | solution.py:22
  1134.1 11.7 cholesky.164
  1145.8 9.8 custom-call.15
  1156.1 11.7 cholesky.181
  1167.9 0.6 compare_reduce_fusion
  1168.5 0.6 compare_reduce_fusion.1
  1170.4 3.8 while.24
  1171.0 1.3 bitcast_dynamic-update-slice_fusion.5
  1172.9 1.3 bitcast_dynamic-update-slice_fusion.5
  1174.2 19.7 %custom-call.16 = f32[2,128,128]{1,2,0:T(8,128)S(1)} custom-call(f32[2,128,128]{2,1,0:T(8,128)S(1)} %get-tuple-element.216), custom_call_target="InvertDiagBlocksLowerTriangular" | custom-call | tf_op jit(solution)/shard_map/while/body/eval_jaxpr/cond/branch_1_fun/jit(_solve_triangular)/triangular_solve | solution.py:25
  1194.8 0.7 copy-done.3
  1196.0 0.8 copy-done.4
  1197.6 1.3 collective-permute-start
  1198.9 7.0 collective-permute-done
  1205.9 0.8 copy-done.2
  (102 shorter events, 16.1 us)
Async XLA Ops:
  0.7 1.2 copy-start
  0.7 1.4 copy-start.1
  2.1 9.9 collective-permute-start
  12.0 9.1 collective-permute-start
  21.1 8.8 collective-permute-start
  29.9 8.9 collective-permute-start
  38.8 9.2 collective-permute-start
  48.0 9.2 collective-permute-start
  57.1 880.0 %collective-permute-start = (f32[256,256]{0,1:T(8,128)S(1)}, f32[256,256]{0,1:T(8,128)S(1)}, u32[]{:S(2)}, u32[]{:S(2)}) collective-permute-start(f32[256,256]{0,1:T(8,128)S(1)} %get-tuple-element.459), channel_id=1, source_target_pairs={{0,1},{1,2},{2,3},{3,4},{4,5},{5,6},{6,7},{8,9},{9,10},{10,11},{11... | collective-permute-start | bytes 786440 | tf_op jit(solution)/shard_map/while/body/eval_jaxpr/ppermute | solution.py:12
  1059.6 1.0 copy-start.3
  1061.2 0.8 copy-start.4
  1062.8 9.2 collective-permute-start
  1194.5 1.0 copy-start.3
  1196.0 0.8 copy-start.4
  1197.6 8.3 collective-permute-start
  1205.9 0.8 copy-start.2
where the time goes:
time: 1210 us
  waiting for transfers between devices  941 us (78%)
  other arithmetic  216 us (18%)
  local copies, waits for them, and re-layouts  20.9 us (2%)
    ppermute x9, waiting for transfers between devices, shifted(): return lax.ppermute(block, axis, route)  941 us
    another operation x14, other arithmetic, qfactor(): lower_second = jnp.linalg.cholesky(gram_second)  69.2 us
    another operation x12, other arithmetic, qfactor(): lower_first = jnp.linalg.cholesky(gram_first)  67.9 us
    another operation x6, other arithmetic, qfactor(): jax.scipy.linalg.solve_triangular(lower_first, panel_now.T, lower=True)  39.4 us
    another operation x4, other arithmetic, qfactor(): jax.scipy.linalg.solve_triangular(lower_second, first_pass.T, lower=True)  39.4 us
  transfers between devices with their start and end apart: 9, of which 9 were waited for; matrix products, arithmetic and copies ran while one was open for 0% of the time, Pallas kernels for 0%

commit v1 on v0

--- a/solution.py
+++ b/solution.py
@@ -1,9 +1,134 @@
 import jax
 import jax.numpy as jnp
 from jax import lax
+from jax.experimental import pallas as pl
+from jax.experimental.pallas import tpu as pltpu
 from jax.sharding import PartitionSpec as P
 
 highest = lax.Precision.HIGHEST
+f32, bf16 = jnp.float32, jnp.bfloat16
+
+DAMP, COARSE, FINE = 5.0, 0.5, 2e-3
+COARSE_STEPS, FINE_STEPS = 48, 8
+BELOW = 5e-5
+
+
+def split(value):
+    high = value.astype(bf16)
+    return high, (value - high.astype(f32)).astype(bf16)
+
+
+def dot_nn(left, right):
+    return lax.dot_general(left, right, (((1,), (0,)), ((), ())), preferred_element_type=f32)
+
+
+def dot_nt(left, right):
+    return lax.dot_general(left, right, (((1,), (1,)), ((), ())), preferred_element_type=f32)
+
+
+def fine_dot(dot, left, right):
+    left_high, left_low = split(left)
+    right_high, right_low = split(right)
+    return dot(left_high, right_high) + (dot(left_high, right_low) + dot(left_low, right_high))
+
+
+def newton_kernel(panel_ref, factor_ref, error_ref, tri_ref):
+    count, order = panel_ref.shape[0], panel_ref.shape[1]
+    rows = lax.broadcasted_iota(jnp.int32, (order, order), 0)
+    cols = lax.broadcasted_iota(jnp.int32, (order, order), 1)
+    eye = (rows == cols).astype(f32)
+    half = jnp.where(rows > cols, 1.0, 0.5 * eye).astype(f32)
+
+    for m in range(count):
+        panel = panel_ref[m]
+        scale = lax.rsqrt(jnp.sum(panel * panel, axis=1, keepdims=True))
+        factor_ref[m] = panel * scale
+        tri_ref[m] = eye * scale
+
+    def coarse(carried):
+        step, worst = carried
+        worst = jnp.float32(0.0)
+        for m in range(count):
+            near = factor_ref[m].astype(bf16)
+            lower = (dot_nt(near, near) - eye) * half
+            size2 = jnp.sum(lower * lower)
+            move = (lower * jnp.minimum(1.0, DAMP * lax.rsqrt(size2))).astype(bf16)
+            factor_ref[m] -= dot_nn(move, near)
+            tri_ref[m] -= dot_nn(move, tri_ref[m].astype(bf16))
+            worst = jnp.maximum(worst, 2.0 * size2)
+        return step + 1, worst
+
+    lax.while_loop(
+        lambda c: (c[0] < COARSE_STEPS) & (c[1] > COARSE * COARSE), coarse, (jnp.int32(0), jnp.float32(1e9))
+    )
+    for m in range(count):
+        factor_ref[m] = fine_dot(dot_nn, tri_ref[m], panel_ref[m])
+
+    def fine(carried):
+        step, worst = carried
+        worst = jnp.float32(0.0)
+        for m in range(count):
+            near = factor_ref[m]
+            lower = (fine_dot(dot_nt, near, near) - eye) * half
+            factor_ref[m] = near - fine_dot(dot_nn, lower, near)
+            worst = jnp.maximum(worst, 2.0 * jnp.sum(lower * lower))
+        return step + 1, worst
+
+    _, worst = lax.while_loop(
+        lambda c: (c[0] < FINE_STEPS) & (c[1] > FINE * FINE), fine, (jnp.int32(0), jnp.float32(1e9))
+    )
+    error_ref[...] = jnp.full(error_ref.shape, worst, f32)
+
+
+def orthogonal_rows(panel):
+    return pl.pallas_call(
+        newton_kernel,
+        out_shape=(jax.ShapeDtypeStruct(panel.shape, f32), jax.ShapeDtypeStruct((8, 128), f32)),
+        in_specs=[pl.BlockSpec(memory_space=pltpu.VMEM)],
+        out_specs=(pl.BlockSpec(memory_space=pltpu.VMEM), pl.BlockSpec(memory_space=pltpu.VMEM)),
+        scratch_shapes=[pltpu.VMEM(panel.shape, f32)],
+        cost_estimate=pl.CostEstimate(flops=10**9, bytes_accessed=10**6, transcendentals=0),
+    )(panel)
+
+
+def close_dot(spec, left, right):
+    return jnp.einsum(spec, left, right, precision=lax.Precision.HIGH, preferred_element_type=f32)
+
+
+def prefix_sweep(diagonal, coupling):
+    count = lax.axis_size("row")
+    position = lax.axis_index("row")
+    order = coupling.shape[-1]
+    product_t = jnp.swapaxes(coupling, -1, -2)
+    reach = 1
+    while reach < count:
+        before = shifted(product_t, "row", reach)
+        product_t = jnp.where(position >= reach, close_dot("bij,bjk->bik", before, product_t), product_t)
+        reach *= 2
+    factor_t, error = orthogonal_rows(product_t)
+    eye = jnp.broadcast_to(jnp.eye(order, dtype=f32), factor_t.shape)
+    before = jnp.where(position == 0, eye, shifted(factor_t, "row", 1))
+    turned = close_dot("bij,bjk->bik", factor_t, coupling)
+    new_diag = close_dot("bij,bkj->bik", close_dot("bij,bjk->bik", factor_t, diagonal), factor_t)
+    full = close_dot("bij,bkj->bik", turned, before)
+    upper = jnp.triu(full)
+    below2 = jnp.sum((full - upper) ** 2)
+    all2 = jnp.sum(full**2)
+    sound = (error[0, 0] <= FINE * FINE) & (below2 <= BELOW * BELOW * all2)
+    sound = sound & jnp.all(jnp.diagonal(full, axis1=-2, axis2=-1) > 0.0)
+    return new_diag, upper, 1.0 - sound.astype(f32), below2 / all2, error[0, 0]
+
+
+def shards(diag_blocks, coupling_blocks):
+    if diag_blocks.shape[2] != 1:
+        return chain(diag_blocks, coupling_blocks)
+    new_diag, upper, fault, _, _ = prefix_sweep(diag_blocks[0, :, 0], coupling_blocks[0, :, 0])
+    faults = lax.psum(fault, ("section", "row"))
+    return lax.cond(
+        faults == 0.0,
+        lambda: (new_diag[None, :, None], upper[None, :, None]),
+        lambda: chain(diag_blocks, coupling_blocks),
+    )
 
 
 def shifted(block, axis, distance):
@@ -38,7 +163,7 @@
     return shifted(outgoing, "row", 1)
 
 
-def shards(diag_blocks, coupling_blocks):
+def chain(diag_blocks, coupling_blocks):
     diagonal = diag_blocks[0]
     coupling = coupling_blocks[0]
     batch_count = diagonal.shape[0]

time: 1210 us -> 157 us (0.13)
  the two profiles are of different devices: /device:TPU:26 before, /device:TPU:0 now
where the time goes in v1:
time: 157 us; the launch traced here: 156 us
  blocking collectives  58.5 us (37%)
  waiting for transfers between devices  33.9 us (22%)
  local copies, waits for them, and re-layouts  21.3 us (14%)
  starting transfers between devices  19 us (12%)
  matrix products  10.4 us (7%)
  Pallas kernels  7.71 us (5%)
  between operations  4.29 us (3%)
    psum x1, blocking collectives, shards(): faults = lax.psum(fault, ('section', 'row'))  58.5 us
    ppermute x4, waiting for transfers between devices, shifted(): return lax.ppermute(block, axis, route)  33.9 us
    ppermute x4, starting transfers between devices, shifted(): return lax.ppermute(block, axis, route)  19 us
    dot_general x1, local copies, waits for them, and re-layouts, close_dot(): jnp.einsum(spec, left, right, precision=lax.Precision.HIGH, preferred_ele...  16.4 us
    dot_general x7, matrix products, close_dot(): jnp.einsum(spec, left, right, precision=lax.Precision.HIGH, preferred_ele...  10.4 us
    pallas_call x1, Pallas kernels, orthogonal_rows(): pl.pallas_call(newton_kernel, out_shape=(jax.ShapeDtypeStruct(panel.shape...  7.71 us
  transfers between devices with their start and end apart: 4, of which 4 were waited for; matrix products, arithmetic and copies ran while one was open for 3% of the time, Pallas kernels for 0%

profile of v1, /device:TPU:0, one launch (start us, length us, event | category | flops | bytes accessed | tf_op | source)
XLA Modules:
  0.0 156.2 jit_solution(11392054929330451523)
XLA Ops:
  0.6 0.0 copy-start
  0.6 0.0 copy-start.1
  0.7 1.3 copy.21
  2.0 4.9 %collective-permute-start.1 = (f32[2,256,256]{2,1,0:T(8,128)S(1)}, f32[2,256,256]{2,1,0:T(8,128)S(1)}, u32[]{:S(2)}, u32[]{:S(2)}) collective-permute-start(f32[2,256,256]{2,1,0:T(8,128)S(1)} %bitcast.126), channel_id=1, source_target_pairs={{0,1},{1,2},{2,3},{3,4},{4,5},{5,6},{6,7},{8,9},{9,10},{10,11},{11... | collective-permute-start | bytes 1572872 | tf_op jit(solution)/shard_map/ppermute | solution.py:137
  6.9 11.1 %collective-permute-done.1 = f32[2,256,256]{2,1,0:T(8,128)S(1)} collective-permute-done((f32[2,256,256]{2,1,0:T(8,128)S(1)}, f32[2,256,256]{2,1,0:T(8,128)S(1)}, u32[]{:S(2)}, u32[]{:S(2)}) %collective-permute-start.1) | collective-permute-done | bytes 524320 | tf_op jit(solution)/shard_map/ppermute | solution.py:137
  18.0 1.4 convolution_select_fusion.3
  19.5 5.4 %collective-permute-start.2 = (f32[2,256,256]{2,1,0:T(8,128)S(1)}, f32[2,256,256]{2,1,0:T(8,128)S(1)}, u32[]{:S(2)}, u32[]{:S(2)}) collective-permute-start(f32[2,256,256]{2,1,0:T(8,128)S(1)} %convolution_select_fusion.3), channel_id=1, source_target_pairs={{0,2},{1,3},{2,4},{3,5},{4,6},{5,7},{8,10},{9,11},{10,12},{11,13},... | collective-permute-start | bytes 1572872 | tf_op jit(solution)/shard_map/ppermute | solution.py:137
  24.9 10.3 %collective-permute-done.2 = f32[2,256,256]{2,1,0:T(8,128)S(1)} collective-permute-done((f32[2,256,256]{2,1,0:T(8,128)S(1)}, f32[2,256,256]{2,1,0:T(8,128)S(1)}, u32[]{:S(2)}, u32[]{:S(2)}) %collective-permute-start.2) | collective-permute-done | bytes 524320 | tf_op jit(solution)/shard_map/ppermute | solution.py:137
  35.2 0.4 convolution_select_fusion.2
  35.6 5.4 %collective-permute-start.3 = (f32[2,256,256]{2,1,0:T(8,128)S(1)}, f32[2,256,256]{2,1,0:T(8,128)S(1)}, u32[]{:S(2)}, u32[]{:S(2)}) collective-permute-start(f32[2,256,256]{2,1,0:T(8,128)S(1)} %convolution_select_fusion.2), channel_id=1, source_target_pairs={{0,4},{1,5},{2,6},{3,7},{8,12},{9,13},{10,14},{11,15},{16,20},{17,... | collective-permute-start | bytes 1572872 | tf_op jit(solution)/shard_map/ppermute | solution.py:137
  41.0 0.1 iota_compare_fusion.3
  41.1 9.3 %collective-permute-done.3 = f32[2,256,256]{2,1,0:T(8,128)S(1)} collective-permute-done((f32[2,256,256]{2,1,0:T(8,128)S(1)}, f32[2,256,256]{2,1,0:T(8,128)S(1)}, u32[]{:S(2)}, u32[]{:S(2)}) %collective-permute-start.3) | collective-permute-done | bytes 524320 | tf_op jit(solution)/shard_map/ppermute | solution.py:137
  50.5 1.2 convolution_select_fusion.1.panel_ref
  51.7 7.7 %shard_map.45 = (f32[2,256,256]{2,1,0:T(8,128)}, f32[8,128]{1,0:T(8,128)}) custom-call(f32[2,256,256]{2,1,0:T(8,128)} %convolution_select_fusion.1.panel_ref), custom_call_target="tpu_custom_call" | custom-call | flops 1000000000 | bytes 1000000 | tf_op jit(solution)/shard_map/pallas_call | solution.py:84
  59.4 1.6 %fusion.50 = f32[2,256,256]{2,1,0:T(8,128)S(1)} fusion(f32[2,256,256]{2,1,0:T(8,128)} %get-tuple-element.214, f32[1,2,1,256,256]{4,3,2,1,0:T(8,128)} %param.12), kind=kOutput, calls=%fused_computation.86 | convolution fusion | flops 201326592 | bytes 1572864 | tf_op jit(solution)/shard_map/bij,bjk->bik/dot_general | solution.py:95
  61.0 3.3 %collective-permute-start.4 = (f32[2,256,256]{2,1,0:T(8,128)}, f32[2,256,256]{2,1,0:T(8,128)S(1)}, u32[]{:S(2)}, u32[]{:S(2)}) collective-permute-start(f32[2,256,256]{2,1,0:T(8,128)} %get-tuple-element.214), channel_id=1, source_target_pairs={{0,1},{1,2},{2,3},{3,4},{4,5},{5,6},{6,7},{8,9},{9,10},{10,11},{11... | collective-permute-start | bytes 1572872 | tf_op jit(solution)/shard_map/ppermute | solution.py:137
  64.3 1.2 slice.36
  66.1 1.6 %fusion.48 = f32[2,256,256]{2,1,0:T(8,128)S(1)} fusion(f32[2,256,256]{2,1,0:T(8,128)} %get-tuple-element.214, f32[1,2,1,256,256]{4,3,2,1,0:T(8,128)} %param.11), kind=kOutput, calls=%fused_computation.84 | convolution fusion | flops 201326592 | bytes 1572864 | tf_op jit(solution)/shard_map/bij,bjk->bik/dot_general | solution.py:95
  67.7 2.3 %fusion.61 = f32[2,256,256]{2,1,0:T(8,128)} fusion(f32[2,256,256]{2,1,0:T(8,128)S(1)} %fusion.48, f32[2,256,256]{2,1,0:T(8,128)} %get-tuple-element.214), kind=kOutput, calls=%fused_computation.105 | convolution fusion | flops 201326592 | bytes 1572864 | tf_op jit(solution)/shard_map/bij,bkj->bik/dot_general | solution.py:95
  70.0 3.2 %collective-permute-done.4 = f32[2,256,256]{2,1,0:T(8,128)S(1)} collective-permute-done((f32[2,256,256]{2,1,0:T(8,128)}, f32[2,256,256]{2,1,0:T(8,128)S(1)}, u32[]{:S(2)}, u32[]{:S(2)}) %collective-permute-start.4) | collective-permute-done | bytes 524320 | tf_op jit(solution)/shard_map/ppermute | solution.py:137
  73.2 1.9 %multiply_reduce_fusion = (f32[]{:T(128)}, f32[]{:T(128)}, f32[2,256,256]{2,1,0:T(8,128)}, f32[2,256,256]{2,1,0:T(8,128)S(1)}) fusion(pred[256,256]{1,0:T(8,128)(4,1)S(1)} %get-tuple-element.311, f32[2,256,256]{2,1,0:T(8,128)S(1)} %fusion.50, f32[2,256,256]{2,1,0:T(8,128)S(1)} %collective-permute-done.4, f32[256,256]{1,0:T(8,128)S(1)} %get-tuple-element.312, ...), kind=kOutput, calls=%fused_computation.89 | convolution fusion | flops 202244096 | bytes 2424841 | tf_op jit(solution)/shard_map/bij,bkj->bik/dot_general | solution.py:95
  75.1 16.4 %copy.23 = f32[2,256,256]{0,2,1:T(8,128)} copy(f32[2,256,256]{2,1,0:T(8,128)S(1)} %get-tuple-element.310) | data formatting | bytes 1048576 | tf_op jit(solution)/shard_map/bij,bkj->bik/dot_general | solution.py:95
  91.5 2.3 %gather_fusion = f32[256,2]{1,0:T(8,128)S(1)} fusion(f32[2,256,256]{0,2,1:T(8,128)} %copy.23, s32[256]{0:T(256)S(1)} %bitcast.124), kind=kCustom, calls=%fused_computation | custom fusion | bytes 6144 | tf_op jit(solution)/shard_map/jit(diagonal)/gather | solution.py:118
  93.9 0.7 compare_reduce_fusion.4
  96.6 58.5 %psum.7 = f32[]{:T(128)} all-reduce(f32[]{:T(128)S(6)} %sub.14), channel_id=1, replica_groups=mesh['section'=4,'row'=8] {'section','row'}, use_global_device_ids=true, to_apply=%region_3.4 | all-reduce | flops 1 | bytes 8 | tf_op jit(solution)/shard_map/psum | solution.py:126
  155.8 0.0 copy-done
  155.8 0.0 copy-done.1
  155.8 0.2 conditional.2
  (2 shorter events, 0.0 us)
Async XLA Ops:
  0.6 155.2 %copy-start = (f32[1,2,1,256,256]{4,3,2,1,0:T(8,128)S(1)}, f32[1,2,1,256,256]{4,3,2,1,0:T(8,128)}, u32[]{:S(2)}) copy-start(f32[1,2,1,256,256]{4,3,2,1,0:T(8,128)} %param.12) | copy-start | bytes 1572868
  0.6 155.2 %copy-start.1 = (f32[1,2,1,256,256]{4,3,2,1,0:T(8,128)S(1)}, f32[1,2,1,256,256]{4,3,2,1,0:T(8,128)}, u32[]{:S(2)}) copy-start(f32[1,2,1,256,256]{4,3,2,1,0:T(8,128)} %param.11) | copy-start | bytes 1572868
  2.0 16.0 %collective-permute-start.1 = (f32[2,256,256]{2,1,0:T(8,128)S(1)}, f32[2,256,256]{2,1,0:T(8,128)S(1)}, u32[]{:S(2)}, u32[]{:S(2)}) collective-permute-start(f32[2,256,256]{2,1,0:T(8,128)S(1)} %bitcast.126), channel_id=1, source_target_pairs={{0,1},{1,2},{2,3},{3,4},{4,5},{5,6},{6,7},{8,9},{9,10},{10,11},{11... | collective-permute-start | bytes 1572872 | tf_op jit(solution)/shard_map/ppermute | solution.py:137
  19.5 15.7 %collective-permute-start.2 = (f32[2,256,256]{2,1,0:T(8,128)S(1)}, f32[2,256,256]{2,1,0:T(8,128)S(1)}, u32[]{:S(2)}, u32[]{:S(2)}) collective-permute-start(f32[2,256,256]{2,1,0:T(8,128)S(1)} %convolution_select_fusion.3), channel_id=1, source_target_pairs={{0,2},{1,3},{2,4},{3,5},{4,6},{5,7},{8,10},{9,11},{10,12},{11,13},... | collective-permute-start | bytes 1572872 | tf_op jit(solution)/shard_map/ppermute | solution.py:137
  35.6 14.9 %collective-permute-start.3 = (f32[2,256,256]{2,1,0:T(8,128)S(1)}, f32[2,256,256]{2,1,0:T(8,128)S(1)}, u32[]{:S(2)}, u32[]{:S(2)}) collective-permute-start(f32[2,256,256]{2,1,0:T(8,128)S(1)} %convolution_select_fusion.2), channel_id=1, source_target_pairs={{0,4},{1,5},{2,6},{3,7},{8,12},{9,13},{10,14},{11,15},{16,20},{17,... | collective-permute-start | bytes 1572872 | tf_op jit(solution)/shard_map/ppermute | solution.py:137
  61.0 12.2 %collective-permute-start.4 = (f32[2,256,256]{2,1,0:T(8,128)}, f32[2,256,256]{2,1,0:T(8,128)S(1)}, u32[]{:S(2)}, u32[]{:S(2)}) collective-permute-start(f32[2,256,256]{2,1,0:T(8,128)} %get-tuple-element.214), channel_id=1, source_target_pairs={{0,1},{1,2},{2,3},{3,4},{4,5},{5,6},{6,7},{8,9},{9,10},{10,11},{11... | collective-permute-start | bytes 1572872 | tf_op jit(solution)/shard_map/ppermute | solution.py:137

commit v2 on v1

--- a/solution.py
+++ b/solution.py
@@ -7,6 +7,8 @@
 
 highest = lax.Precision.HIGHEST
 f32, bf16 = jnp.float32, jnp.bfloat16
+MESH = pl.DeviceIdType.MESH
+CHUNK = 32
 
 DAMP, COARSE, FINE = 5.0, 0.5, 2e-3
 COARSE_STEPS, FINE_STEPS = 48, 8
@@ -91,41 +93,211 @@
     )(panel)
 
 
-def close_dot(spec, left, right):
-    return jnp.einsum(spec, left, right, precision=lax.Precision.HIGH, preferred_element_type=f32)
-
-
-def prefix_sweep(diagonal, coupling):
-    count = lax.axis_size("row")
+def neighbours_ready(position, count):
+    barrier = pltpu.get_barrier_semaphore()
+    for away in (1, count - 1):
+        peer = {"row": lax.rem(position + away, count)}
+        pl.semaphore_signal(barrier, inc=1, device_id=peer, device_id_type=MESH)
+    pl.semaphore_wait(barrier, 2)
+
+
+def product_kernel(count, coupling_ref, product_ref, inbox, high_ref, low_ref, send_sem, recv_sem):
     position = lax.axis_index("row")
-    order = coupling.shape[-1]
-    product_t = jnp.swapaxes(coupling, -1, -2)
-    reach = 1
-    while reach < count:
-        before = shifted(product_t, "row", reach)
-        product_t = jnp.where(position >= reach, close_dot("bij,bjk->bik", before, product_t), product_t)
-        reach *= 2
-    factor_t, error = orthogonal_rows(product_t)
-    eye = jnp.broadcast_to(jnp.eye(order, dtype=f32), factor_t.shape)
-    before = jnp.where(position == 0, eye, shifted(factor_t, "row", 1))
-    turned = close_dot("bij,bjk->bik", factor_t, coupling)
-    new_diag = close_dot("bij,bkj->bik", close_dot("bij,bjk->bik", factor_t, diagonal), factor_t)
-    full = close_dot("bij,bkj->bik", turned, before)
-    upper = jnp.triu(full)
-    below2 = jnp.sum((full - upper) ** 2)
-    all2 = jnp.sum(full**2)
-    sound = (error[0, 0] <= FINE * FINE) & (below2 <= BELOW * BELOW * all2)
-    sound = sound & jnp.all(jnp.diagonal(full, axis1=-2, axis2=-1) > 0.0)
-    return new_diag, upper, 1.0 - sound.astype(f32), below2 / all2, error[0, 0]
+    batch, order = coupling_ref.shape[0], coupling_ref.shape[1]
+    chunks = order // CHUNK
+    neighbours_ready(position, count)
+
+    @pl.when(position == 0)
+    def _():
+        rows = lax.broadcasted_iota(jnp.int32, (order, order), 0)
+        cols = lax.broadcasted_iota(jnp.int32, (order, order), 1)
+        for m in range(batch):
+            inbox[m] = (rows == cols).astype(f32)
+
+    for m in range(batch):
+        high_ref[m], low_ref[m] = split(coupling_ref[m])
+
+    def passing(step):
+        m, rows = lax.div(step, chunks), pl.ds(pl.multiple_of(lax.rem(step, chunks) * CHUNK, CHUNK), CHUNK)
+        copy = pltpu.make_async_remote_copy(
+            src_ref=product_ref.at[m, rows],
+            dst_ref=inbox.at[m, rows],
+            send_sem=send_sem.at[step],
+            recv_sem=recv_sem.at[step],
+            device_id={"row": lax.rem(position + 1, count)},
+            device_id_type=MESH,
+        )
+        return m, rows, copy
+
+    def forward(step, unused):
+        m, rows, copy = passing(step)
+
+        @pl.when(position > 0)
+        def _():
+            copy.wait_recv()
+
+        high, low = split(inbox[m, rows])
+        product_ref[m, rows] = dot_nt(high, high_ref[m]) + (dot_nt(high, low_ref[m]) + dot_nt(low, high_ref[m]))
+
+        @pl.when(position < count - 1)
+        def _():
+            copy.start()
+
+        return unused
+
+    def sent(step, unused):
+        @pl.when(position < count - 1)
+        def _():
+            passing(step)[2].wait_send()
+
+        return unused
+
+    lax.fori_loop(0, batch * chunks, forward, 0)
+    lax.fori_loop(0, batch * chunks, sent, 0)
+
+
+def prefix_product(coupling):
+    count, steps = lax.axis_size("row"), coupling.shape[0] * (coupling.shape[1] // CHUNK)
+    return pl.pallas_call(
+        lambda *refs: product_kernel(count, *refs),
+        out_shape=jax.ShapeDtypeStruct(coupling.shape, f32),
+        in_specs=[pl.BlockSpec(memory_space=pltpu.VMEM)],
+        out_specs=pl.BlockSpec(memory_space=pltpu.VMEM),
+        scratch_shapes=[
+            pltpu.VMEM(coupling.shape, f32),
+            pltpu.VMEM(coupling.shape, bf16),
+            pltpu.VMEM(coupling.shape, bf16),
+            pltpu.SemaphoreType.DMA((steps,)),
+            pltpu.SemaphoreType.DMA((steps,)),
+        ],
+        compiler_params=pltpu.CompilerParams(collective_id=0, has_side_effects=True),
+    )(coupling)
+
+
+def finish_kernel(
+    count, sections, factor_ref, coupling_ref, diag_ref, error_ref, new_ref, upper_ref, fault_ref,
+    before, own_fault, row_fault, row_box, section_box, send_sem, recv_sem, flag_send, flag_recv,
+):
+    position, section = lax.axis_index("row"), lax.axis_index("section")
+    batch, order = coupling_ref.shape[0], coupling_ref.shape[1]
+    barrier = pltpu.get_barrier_semaphore()
+    for k in range(1, count):
+        peer = {"row": lax.rem(position + k, count)}
+        pl.semaphore_signal(barrier, inc=1, device_id=peer, device_id_type=MESH)
+    for k in range(1, sections):
+        peer = {"section": lax.rem(section + k, sections)}
+        pl.semaphore_signal(barrier, inc=1, device_id=peer, device_id_type=MESH)
+    pl.semaphore_wait(barrier, count + sections - 2)
+
+    copies = [
+        pltpu.make_async_remote_copy(
+            src_ref=factor_ref.at[m],
+            dst_ref=before.at[m],
+            send_sem=send_sem.at[m],
+            recv_sem=recv_sem.at[m],
+            device_id={"row": lax.rem(position + 1, count)},
+            device_id_type=MESH,
+        )
+        for m in range(batch)
+    ]
+
+    @pl.when(position < count - 1)
+    def _():
+        for copy in copies:
+            copy.start()
+
+    rows = lax.broadcasted_iota(jnp.int32, (order, order), 0)
+    cols = lax.broadcasted_iota(jnp.int32, (order, order), 1)
+
+    @pl.when(position == 0)
+    def _():
+        for m in range(batch):
+            before[m] = (rows == cols).astype(f32)
+
+    for m in range(batch):
+        upper_ref[m] = fine_dot(dot_nn, factor_ref[m], coupling_ref[m])
+        new_ref[m] = fine_dot(dot_nt, fine_dot(dot_nn, factor_ref[m], diag_ref[m]), factor_ref[m])
+
+    bad = jnp.where(error_ref[...] <= FINE * FINE, 0.0, 1.0)
+    for m in range(batch):
+
+        @pl.when(position > 0)
+        def _():
+            copies[m].wait_recv()
+
+        full = fine_dot(dot_nt, upper_ref[m], before[m])
+        upper_ref[m] = jnp.where(rows <= cols, full, 0.0)
+        squares = full * full
+        below2 = jnp.sum(jnp.where(rows > cols, squares, 0.0), axis=(0, 1), keepdims=True)
+        all2 = jnp.sum(squares, axis=(0, 1), keepdims=True)
+        least = jnp.min(jnp.where(rows == cols, full, jnp.inf), axis=(0, 1), keepdims=True)
+        bad += jnp.where((below2 <= BELOW * BELOW * all2) & (least > 0.0), 0.0, 1.0)
+    own_fault[...] = bad
+
+    def exchange(source, box, axis, here, size, first):
+        sends = [
+            pltpu.make_async_remote_copy(
+                src_ref=source,
+                dst_ref=box.at[k - 1],
+                send_sem=flag_send.at[first + k - 1],
+                recv_sem=flag_recv.at[first + k - 1],
+                device_id={axis: lax.rem(here + k, size)},
+                device_id_type=MESH,
+            )
+            for k in range(1, size)
+        ]
+        for send in sends:
+            send.start()
+        for send in sends:
+            send.wait()
+        return source[...] + sum(box[k] for k in range(size - 1))
+
+    row_fault[...] = exchange(own_fault, row_box, "row", position, count, 0)
+    fault_ref[...] = exchange(row_fault, section_box, "section", section, sections, count - 1)
+
+    @pl.when(position < count - 1)
+    def _():
+        for copy in copies:
+            copy.wait_send()
+
+
+def finish(factor, coupling, diagonal, error):
+    count, sections = lax.axis_size("row"), lax.axis_size("section")
+    batch = coupling.shape[0]
+    flags = count + sections - 2
+    vmem = pl.BlockSpec(memory_space=pltpu.VMEM)
+    return pl.pallas_call(
+        lambda *refs: finish_kernel(count, sections, *refs),
+        out_shape=(
+            jax.ShapeDtypeStruct(coupling.shape, f32),
+            jax.ShapeDtypeStruct(coupling.shape, f32),
+            jax.ShapeDtypeStruct(error.shape, f32),
+        ),
+        in_specs=[vmem] * 4,
+        out_specs=(vmem, vmem, vmem),
+        scratch_shapes=[
+            pltpu.VMEM(coupling.shape, f32),
+            pltpu.VMEM(error.shape, f32),
+            pltpu.VMEM(error.shape, f32),
+            pltpu.VMEM((count - 1, *error.shape), f32),
+            pltpu.VMEM((sections - 1, *error.shape), f32),
+            pltpu.SemaphoreType.DMA((batch,)),
+            pltpu.SemaphoreType.DMA((batch,)),
+            pltpu.SemaphoreType.DMA((flags,)),
+            pltpu.SemaphoreType.DMA((flags,)),
+        ],
+        compiler_params=pltpu.CompilerParams(collective_id=1, has_side_effects=True),
+    )(factor, coupling, diagonal, error)
 
 
 def shards(diag_blocks, coupling_blocks):
     if diag_blocks.shape[2] != 1:
         return chain(diag_blocks, coupling_blocks)
-    new_diag, upper, fault, _, _ = prefix_sweep(diag_blocks[0, :, 0], coupling_blocks[0, :, 0])
-    faults = lax.psum(fault, ("section", "row"))
+    diagonal, coupling = diag_blocks[0, :, 0], coupling_blocks[0, :, 0]
+    factor, error = orthogonal_rows(prefix_product(coupling))
+    new_diag, upper, faults = finish(factor, coupling, diagonal, error)
     return lax.cond(
-        faults == 0.0,
+        faults[0, 0] == 0.0,
         lambda: (new_diag[None, :, None], upper[None, :, None]),
         lambda: chain(diag_blocks, coupling_blocks),
     )
@@ -142,14 +314,12 @@
 
 
 def qfactor(panel_now):
-    gram_first = product(panel_now.T, panel_now)
-    lower_first = jnp.linalg.cholesky(gram_first)
-    first_pass = jax.scipy.linalg.solve_triangular(lower_first, panel_now.T, lower=True).T
-    gram_second = product(first_pass.T, first_pass)
-    lower_second = jnp.linalg.cholesky(gram_second)
-    orthogonal = jax.scipy.linalg.solve_triangular(lower_second, first_pass.T, lower=True).T
-    upper_part = product(lower_second.T, lower_first.T)
-    return (orthogonal, upper_part)
+    def one_pass(_, carried):
+        panel, upper = carried
+        lower = jnp.linalg.cholesky(product(panel.T, panel))
+        return jax.scipy.linalg.solve_triangular(lower, panel.T, lower=True).T, product(lower.T, upper)
+
+    return lax.fori_loop(0, 2, one_pass, (panel_now, jnp.eye(panel_now.shape[0], dtype=f32)))
 
 
 def segment(panel_now, diagonal):

time: 157 us -> 81.8 us (0.52)
  Pallas kernels: 7.71 us -> 74.9 us
  blocking collectives: 58.5 us -> 0 us
  waiting for transfers between devices: 33.9 us -> 0 us
  starting transfers between devices: 19 us -> 0 us
  local copies, waits for them, and re-layouts: 21.3 us -> 4.93 us
  matrix products: 10.4 us -> 0 us
  between operations: 4.29 us -> 1.32 us
    pallas_call x0 -> x2, Pallas kernels: none -> 67.1 us  [the longest x1 47.4 us: finish(): pl.pallas_call(lambda *refs: finish_kernel(count, sections, *refs), out_s...]
    psum x1 -> x0, blocking collectives: 58.5 us -> none  [shards(): faults = lax.psum(fault, ('section', 'row'))]
    ppermute x4 -> x0, waiting for transfers between devices: 33.9 us -> none  [shifted(): return lax.ppermute(block, axis, route)]
    ppermute x4 -> x0, starting transfers between devices: 19 us -> none  [shifted(): return lax.ppermute(block, axis, route)]
    dot_general x1 -> x0, local copies, waits for them, and re-layouts: 16.4 us -> none  [close_dot(): jnp.einsum(spec, left, right, precision=lax.Precision.HIGH, preferred_ele...]
    dot_general x7 -> x0, matrix products: 10.4 us -> none  [close_dot(): jnp.einsum(spec, left, right, precision=lax.Precision.HIGH, preferred_ele...]
    unnamed x5 -> x6, local copies, waits for them, and re-layouts: 1.33 us -> 3.75 us
    gather x1 -> x0, local copies, waits for them, and re-layouts: 2.32 us -> none  [prefix_sweep(): sound = sound & jnp.all(jnp.diagonal(full, axis1=-2, axis2=-1) > 0.0)]
  transfers between devices with their start and end apart: 4 -> 0, of which waited for: 4 -> 0; matrix products, arithmetic and copies ran while one was open for 3% -> 0% of each run, Pallas kernels for 0% -> 0%
where the time goes in v2:
time: 81.8 us; the launch traced here: 81.4 us
  Pallas kernels  74.9 us (92%)
  local copies, waits for them, and re-layouts  4.93 us (6%)
  between operations  1.32 us (2%)
    pallas_call x1, Pallas kernels, finish(): pl.pallas_call(lambda *refs: finish_kernel(count, sections, *refs), out_s...  47.4 us
    pallas_call x1, Pallas kernels, prefix_product(): pl.pallas_call(lambda *refs: product_kernel(count, *refs), out_shape=jax....  19.7 us
    pallas_call x1, Pallas kernels, orthogonal_rows(): pl.pallas_call(newton_kernel, out_shape=(jax.ShapeDtypeStruct(panel.shape...  7.8 us
    unnamed x6, local copies, waits for them, and re-layouts  3.75 us

profile of v2, /device:TPU:0, one launch (start us, length us, event | category | flops | bytes accessed | tf_op | source)
XLA Modules:
  0.0 81.4 jit_solution(5922504426858699887)
XLA Ops:
  0.6 19.7 %shard_map.45.panel_ref = f32[2,256,256]{2,1,0:T(8,128)} custom-call(f32[2,256,256]{2,1,0:T(8,128)} %bitcast.96), custom_call_target="tpu_custom_call" | custom-call | tf_op jit(solution)/shard_map/pallas_call | solution.py:161
  20.3 0.0 copy-start.2
  20.4 0.0 copy-start.3
  20.4 7.8 %shard_map.46 = (f32[2,256,256]{2,1,0:T(8,128)}, f32[8,128]{1,0:T(8,128)}) custom-call(f32[2,256,256]{2,1,0:T(8,128)} %shard_map.45.panel_ref), custom_call_target="tpu_custom_call" | custom-call | flops 1000000000 | bytes 1000000 | tf_op jit(solution)/shard_map/pallas_call | solution.py:86
  28.2 0.0 copy-done.2
  28.2 0.0 copy-done.3
  28.2 47.4 %shard_map.47 = (f32[2,256,256]{2,1,0:T(8,128)}, f32[2,256,256]{2,1,0:T(8,128)}, f32[8,128]{1,0:T(8,128)}) custom-call(f32[2,256,256]{2,1,0:T(8,128)} %get-tuple-element.232.refs_0_, f32[2,256,256]{2,1,0:T(8,128)S(1)} %bitcast.97, f32[2,256,256]{2,1,0:T(8,128)S(1)} %bitcast.99, f32[8,128]{1,0:T(8,128)} %get-tuple-element.233.refs_3_), custom_call_target="tpu_custom_call" | custom-call | tf_op jit(solution)/shard_map/pallas_call | solution.py:269
  75.6 1.2 %slice.50 = f32[1,1]{1,0:T(1,128)} slice(f32[8,128]{1,0:T(8,128)} %get-tuple-element.234), slice={[0:1], [0:1]} | slice | bytes 8 | tf_op jit(solution)/shard_map/slice | solution.py:300
  77.4 0.2 conditional.2
  77.7 1.9 %copy.69 = f32[1,2,1,256,256]{4,3,2,1,0:T(8,128)} copy(f32[1,2,1,256,256]{4,3,2,1,0:T(8,128)} %bitcast.22) | data formatting | bytes 1048576
  79.5 1.9 %copy.70 = f32[1,2,1,256,256]{4,3,2,1,0:T(8,128)} copy(f32[1,2,1,256,256]{4,3,2,1,0:T(8,128)} %bitcast.23) | data formatting | bytes 1048576
Async XLA Ops:
  20.3 7.8 %copy-start.2 = (f32[1,2,1,256,256]{4,3,2,1,0:T(8,128)S(1)}, f32[1,2,1,256,256]{4,3,2,1,0:T(8,128)}, u32[]{:S(2)}) copy-start(f32[1,2,1,256,256]{4,3,2,1,0:T(8,128)} %param.11) | copy-start | bytes 1572868
  20.4 7.8 %copy-start.3 = (f32[1,2,1,256,256]{4,3,2,1,0:T(8,128)S(1)}, f32[1,2,1,256,256]{4,3,2,1,0:T(8,128)}, u32[]{:S(2)}) copy-start(f32[1,2,1,256,256]{4,3,2,1,0:T(8,128)} %param.10) | copy-start | bytes 1572868

commit v3 on v2

--- a/solution.py
+++ b/solution.py
@@ -107,16 +107,6 @@
     chunks = order // CHUNK
     neighbours_ready(position, count)
 
-    @pl.when(position == 0)
-    def _():
-        rows = lax.broadcasted_iota(jnp.int32, (order, order), 0)
-        cols = lax.broadcasted_iota(jnp.int32, (order, order), 1)
-        for m in range(batch):
-            inbox[m] = (rows == cols).astype(f32)
-
-    for m in range(batch):
-        high_ref[m], low_ref[m] = split(coupling_ref[m])
-
     def passing(step):
         m, rows = lax.div(step, chunks), pl.ds(pl.multiple_of(lax.rem(step, chunks) * CHUNK, CHUNK), CHUNK)
         copy = pltpu.make_async_remote_copy(
@@ -131,18 +121,19 @@
 
     def forward(step, unused):
         m, rows, copy = passing(step)
-
-        @pl.when(position > 0)
-        def _():
-            copy.wait_recv()
-
+        copy.wait_recv()
         high, low = split(inbox[m, rows])
-        product_ref[m, rows] = dot_nt(high, high_ref[m]) + (dot_nt(high, low_ref[m]) + dot_nt(low, high_ref[m]))
+        both = dot_nn(jnp.concatenate([high, low], axis=0), high_ref[m])
+        product_ref[m, rows] = both[:CHUNK] + (both[CHUNK:] + dot_nn(high, low_ref[m]))
 
         @pl.when(position < count - 1)
         def _():
             copy.start()
 
+        return unused
+
+    def first(step, unused):
+        passing(step)[2].start()
         return unused
 
     def sent(step, unused):
@@ -152,7 +143,18 @@
 
         return unused
 
-    lax.fori_loop(0, batch * chunks, forward, 0)
+    @pl.when(position == 0)
+    def _():
+        for m in range(batch):
+            product_ref[m] = coupling_ref[m].T
+        lax.fori_loop(0, batch * chunks, first, 0)
+
+    @pl.when(position > 0)
+    def _():
+        for m in range(batch):
+            high_ref[m], low_ref[m] = split(coupling_ref[m].T)
+        lax.fori_loop(0, batch * chunks, forward, 0)
+
     lax.fori_loop(0, batch * chunks, sent, 0)
 
 

time: 81.8 us -> 81 us (level)
  no operation moved by 1% of the time
where the time goes in v3:
time: 81 us; the launch traced here: 80.7 us
  Pallas kernels  74.2 us (92%)
  local copies, waits for them, and re-layouts  4.93 us (6%)
  between operations  1.32 us (2%)
    pallas_call x1, Pallas kernels, finish(): pl.pallas_call(lambda *refs: finish_kernel(count, sections, *refs), out_s...  46.9 us
    pallas_call x1, Pallas kernels, prefix_product(): pl.pallas_call(lambda *refs: product_kernel(count, *refs), out_shape=jax....  19.5 us
    pallas_call x1, Pallas kernels, orthogonal_rows(): pl.pallas_call(newton_kernel, out_shape=(jax.ShapeDtypeStruct(panel.shape...  7.8 us
    unnamed x6, local copies, waits for them, and re-layouts  3.75 us

profile of v3, /device:TPU:0, one launch (start us, length us, event | category | flops | bytes accessed | tf_op | source)
XLA Modules:
  0.0 80.7 jit_solution(14065566730332033678)
XLA Ops:
  0.6 19.5 %shard_map.45.panel_ref = f32[2,256,256]{2,1,0:T(8,128)} custom-call(f32[2,256,256]{2,1,0:T(8,128)} %bitcast.96), custom_call_target="tpu_custom_call" | custom-call | tf_op jit(solution)/shard_map/pallas_call | solution.py:163
  20.2 0.0 copy-start.2
  20.2 0.0 copy-start.3
  20.2 7.8 %shard_map.46 = (f32[2,256,256]{2,1,0:T(8,128)}, f32[8,128]{1,0:T(8,128)}) custom-call(f32[2,256,256]{2,1,0:T(8,128)} %shard_map.45.panel_ref), custom_call_target="tpu_custom_call" | custom-call | flops 1000000000 | bytes 1000000 | tf_op jit(solution)/shard_map/pallas_call | solution.py:86
  28.0 0.0 copy-done.2
  28.0 0.0 copy-done.3
  28.0 46.9 %shard_map.47 = (f32[2,256,256]{2,1,0:T(8,128)}, f32[2,256,256]{2,1,0:T(8,128)}, f32[8,128]{1,0:T(8,128)}) custom-call(f32[2,256,256]{2,1,0:T(8,128)} %get-tuple-element.232.refs_0_, f32[2,256,256]{2,1,0:T(8,128)S(1)} %bitcast.97, f32[2,256,256]{2,1,0:T(8,128)S(1)} %bitcast.99, f32[8,128]{1,0:T(8,128)} %get-tuple-element.233.refs_3_), custom_call_target="tpu_custom_call" | custom-call | tf_op jit(solution)/shard_map/pallas_call | solution.py:271
  74.9 1.2 %slice.50 = f32[1,1]{1,0:T(1,128)} slice(f32[8,128]{1,0:T(8,128)} %get-tuple-element.234), slice={[0:1], [0:1]} | slice | bytes 8 | tf_op jit(solution)/shard_map/slice | solution.py:302
  76.7 0.2 conditional.2
  77.0 1.9 %copy.69 = f32[1,2,1,256,256]{4,3,2,1,0:T(8,128)} copy(f32[1,2,1,256,256]{4,3,2,1,0:T(8,128)} %bitcast.22) | data formatting | bytes 1048576
  78.8 1.9 %copy.70 = f32[1,2,1,256,256]{4,3,2,1,0:T(8,128)} copy(f32[1,2,1,256,256]{4,3,2,1,0:T(8,128)} %bitcast.23) | data formatting | bytes 1048576
Async XLA Ops:
  20.2 7.8 %copy-start.2 = (f32[1,2,1,256,256]{4,3,2,1,0:T(8,128)S(1)}, f32[1,2,1,256,256]{4,3,2,1,0:T(8,128)}, u32[]{:S(2)}) copy-start(f32[1,2,1,256,256]{4,3,2,1,0:T(8,128)} %param.11) | copy-start | bytes 1572868
  20.2 7.8 %copy-start.3 = (f32[1,2,1,256,256]{4,3,2,1,0:T(8,128)S(1)}, f32[1,2,1,256,256]{4,3,2,1,0:T(8,128)}, u32[]{:S(2)}) copy-start(f32[1,2,1,256,256]{4,3,2,1,0:T(8,128)} %param.10) | copy-start | bytes 1572868
